TPU v7x, 16 devices: a whole 2x2x2 slice. The times are simulated.
16 devices in a mesh: dp: 4 (over z, y), sp: 4 (over x, core).
Axes of the slice: x: 2, y: 2, z: 2, core: 2. Of those that a mesh axis runs over, the one named last changes fastest.
Arguments:
- tokens: bfloat16 [1024, 2048], P(('dp', 'sp')), parts along dimension 0
- w_query: bfloat16 [2048, 2048], replicated
- w_key: bfloat16 [2048, 2048], replicated
- w_value: bfloat16 [2048, 2048], replicated
- w_out: bfloat16 [2048, 2048], replicated
- w_gate: bfloat16 [2048, 2048], replicated
- w_up: bfloat16 [2048, 2048], replicated
- w_down: bfloat16 [2048, 2048], replicated
- w_router: bfloat16 [2048, 60], replicated
- expert_ids: int32 [1024, 4], P(('dp', 'sp')), parts along dimension 0
Outputs:
- output 1: bfloat16 [1024, 2048], P(('dp', 'sp')), parts along dimension 0
- output 2: bfloat16 [240, 32, 2048], P(('dp', 'sp')), parts along dimension 0
There are 4 independent parts. A program takes and returns all parts, laid end to end along the dimension named above; an argument that names none is the same for every part.
All inputs are finite; a program needn't handle non-finite values.
Results may differ from a plain program's by a relative error of at most 0.00521.
Values are sent between devices in bfloat16 or wider.
A program may use at most 1 GiB of HBM per device.

v0:
```python
import math
import jax
import jax.numpy as jnp
from jax import lax
from jax.sharding import PartitionSpec as P

HEAD_DIM = 128


def query_block(n_rows, n_heads, seq_len):
    blk_rows = n_rows
    while blk_rows > 8 and blk_rows * n_heads * seq_len > 2 ** 24:
        blk_rows = blk_rows // 2
    return blk_rows


def head_attention(q_rows, k_all, v_all, kv_loc, q_offset):
    n_rows = q_rows.shape[0]
    seq_len = k_all.shape[0]
    q_per_kv = q_rows.shape[1] // (kv_loc * HEAD_DIM)
    blk_rows = query_block(n_rows, kv_loc * q_per_kv, seq_len)
    q_blocks = q_rows.reshape(n_rows // blk_rows, blk_rows, kv_loc, q_per_kv, HEAD_DIM)
    keys_heads = k_all.reshape(seq_len, kv_loc, HEAD_DIM)
    values_heads = v_all.reshape(seq_len, kv_loc, HEAD_DIM)
    key_pos = jnp.arange(seq_len, dtype=jnp.int32)
    inv_scale = 1.0 / math.sqrt(HEAD_DIM)

    def one_block(blk_args):
        q_blk, q_start = blk_args
        scores = jnp.einsum('qkgd,skd->kgqs', q_blk, keys_heads, preferred_element_type=jnp.float32) * inv_scale
        query_pos = q_start + jnp.arange(blk_rows, dtype=jnp.int32)
        scores = jnp.where(query_pos[:, None] >= key_pos[None, :], scores, -jnp.inf)
        attn_probs = jax.nn.softmax(scores, axis=-1).astype(jnp.bfloat16)
        blk_out = jnp.einsum('kgqs,skd->qkgd', attn_probs, values_heads, preferred_element_type=jnp.float32)
        return blk_out.astype(jnp.bfloat16).reshape(blk_rows, kv_loc * q_per_kv * HEAD_DIM)

    starts = q_offset + jnp.arange(n_rows // blk_rows, dtype=jnp.int32) * blk_rows
    return lax.map(one_block, (q_blocks, starts)).reshape(n_rows, kv_loc * q_per_kv * HEAD_DIM)


def shared_expert(hidden, w_gate, w_up, w_down):
    gate_act = jnp.dot(hidden, w_gate, preferred_element_type=jnp.float32)
    up_act = jnp.dot(hidden, w_up, preferred_element_type=jnp.float32)
    swiglu = (jax.nn.silu(gate_act) * up_act).astype(jnp.bfloat16)
    return (hidden.astype(jnp.float32) + jnp.dot(swiglu, w_down, preferred_element_type=jnp.float32)).astype(jnp.bfloat16)


def dispatch_rows(hidden, w_router, expert_ids, capacity):
    tok_rows, hidden_dim = hidden.shape
    n_experts = w_router.shape[1]
    top_k = expert_ids.shape[1]
    logits = jnp.dot(hidden, w_router, preferred_element_type=jnp.float32)
    gate_vals = jax.nn.sigmoid(jnp.take_along_axis(logits, expert_ids, axis=1)).reshape(-1)
    pair_expert = expert_ids.reshape(-1)
    onehot = (pair_expert[:, None] == jnp.arange(n_experts, dtype=jnp.int32)[None, :]).astype(jnp.int32)
    slot_rank = jnp.sum((jnp.cumsum(onehot, axis=0) - onehot) * onehot, axis=1)
    n_slots = n_experts * capacity
    dest_row = jnp.where(slot_rank < capacity, pair_expert * capacity + slot_rank, n_slots)
    pair_token = jnp.arange(tok_rows * top_k, dtype=jnp.int32) // top_k
    slot_token = jax.ops.segment_sum(pair_token, dest_row, num_segments=n_slots)
    slot_gate = jax.ops.segment_sum(gate_vals, dest_row, num_segments=n_slots)
    gathered = jnp.take(hidden, slot_token, axis=0)
    return (gathered.astype(jnp.float32) * slot_gate[:, None]).astype(jnp.bfloat16).reshape(n_experts, capacity, hidden_dim)


def head_columns(proj, kv_heads, n_grp):
    if n_grp <= kv_heads:
        return proj
    tok_rows = proj.shape[0]
    repeated = jnp.repeat(proj.reshape(tok_rows, kv_heads, HEAD_DIM), n_grp // kv_heads, axis=1)
    return repeated.reshape(tok_rows, n_grp * HEAD_DIM)


def solution(mesh):
    n_grp = mesh.shape['sp']
    row_spec = P(('dp', 'sp'), None)
    buf_spec = P(('dp', 'sp'), None, None)
    replicated = P()

    def local_step(tokens, w_query, w_key, w_value, w_out, w_gate, w_up, w_down, w_router, expert_ids):
        tok_rows = tokens.shape[0]
        kv_heads = w_key.shape[1] // HEAD_DIM
        n_experts = w_router.shape[1]
        top_k = expert_ids.shape[1]
        capacity = max(2, (tok_rows * top_k // n_experts) * 2)
        kv_loc = max(kv_heads // n_grp, 1)
        queries = jnp.dot(tokens, w_query, preferred_element_type=jnp.float32).astype(jnp.bfloat16)
        keys_loc = jnp.dot(tokens, w_key, preferred_element_type=jnp.float32).astype(jnp.bfloat16)
        values_loc = jnp.dot(tokens, w_value, preferred_element_type=jnp.float32).astype(jnp.bfloat16)
        q_all = lax.all_to_all(queries, 'sp', 1, 0, tiled=True)
        k_all = lax.all_to_all(head_columns(keys_loc, kv_heads, n_grp), 'sp', 1, 0, tiled=True)
        v_all = lax.all_to_all(head_columns(values_loc, kv_heads, n_grp), 'sp', 1, 0, tiled=True)
        attn_heads = head_attention(q_all, k_all, v_all, kv_loc, 0)
        attn_loc = lax.all_to_all(attn_heads, 'sp', 0, 1, tiled=True)
        hidden = (tokens.astype(jnp.float32) + jnp.dot(attn_loc, w_out, preferred_element_type=jnp.float32)).astype(jnp.bfloat16)
        hidden_out = shared_expert(hidden, w_gate, w_up, w_down)
        send_buf = dispatch_rows(hidden, w_router, expert_ids, capacity)
        expert_buf = lax.all_to_all(send_buf, 'sp', 0, 1, tiled=True)
        return hidden_out, expert_buf

    return jax.shard_map(local_step, mesh=mesh, in_specs=(row_spec, replicated, replicated, replicated, replicated, replicated, replicated, replicated, replicated, row_spec), out_specs=(row_spec, buf_spec), check_vma=False)
```

profile of v0, /device:TPU:0, one launch (start us, length us, event | category | flops | bytes accessed | tf_op | source)
XLA Modules:
  0.0 96.2 jit_solution(10153551348864696774)
XLA Ops:
  0.6 0.0 copy-start
  0.6 0.0 copy-start.2
  0.7 0.0 copy-start.3
  0.7 5.1 %convolution_convert_fusion = bf16[64,2048]{1,0:T(8,128)(2,1)S(1)} fusion(bf16[64,2048]{1,0:T(8,128)(2,1)} %param.10, bf16[2048,2048]{1,0:T(8,128)(2,1)} %param.11), kind=kOutput, calls=%fused_computation.11 | convolution fusion | flops 537001984 | bytes 8912896 | tf_op jit(solution)/shard_map/dot_general | solution.py:87
  5.8 0.7 copy.72
  6.5 4.5 %all-to-all-start.2 = ((bf16[64,4,512]{2,0,1:T(8,128)(2,1)}), bf16[64,4,512]{2,0,1:T(8,128)(2,1)S(1)}, u32[]{:S(2)}, u32[]{:S(2)}) async-start(bf16[64,4,512]{2,0,1:T(8,128)(2,1)} %bitcast.70), calls=%async_computation.2 | async-start | bytes 524288 | tf_op jit(solution)/shard_map/all_to_all | solution.py:90
  11.0 0.0 copy-done.3
  11.0 0.1 copy.43
  11.1 0.1 eq.29
  11.2 0.1 eq.25
  11.3 0.1 copy.46
  11.4 0.1 mul.51
  11.5 0.6 reduce-window.6
  12.2 0.2 slice_reduce_fusion
  12.4 0.1 broadcast_add_fusion
  12.5 0.0 slice-start
  12.5 0.1 copy.45
  12.6 0.0 copy-done.2
  12.6 0.0 slice-start.1
  12.6 5.1 %convolution_convert_fusion.1 = bf16[64,2048]{1,0:T(8,128)(2,1)S(1)} fusion(bf16[64,2048]{1,0:T(8,128)(2,1)S(1)} %copy-done.2, bf16[2048,2048]{1,0:T(8,128)(2,1)} %param.12), kind=kOutput, calls=%fused_computation.12 | convolution fusion | flops 537001984 | bytes 8912896 | tf_op jit(solution)/shard_map/dot_general | solution.py:88
  17.7 0.7 copy.73
  18.5 0.0 slice-done
  18.5 0.0 slice-done.1
  18.5 1.6 %convolution_convert_fusion.2 = bf16[64,2048]{1,0:T(8,128)(2,1)S(1)} fusion(bf16[64,2048]{1,0:T(8,128)(2,1)S(1)} %copy-done.2, bf16[2048,2048]{1,0:T(8,128)(2,1)S(1)} %bitcast.74), kind=kOutput, calls=%fused_computation.13 | convolution fusion | flops 537001984 | bytes 8912896 | tf_op jit(solution)/shard_map/dot_general | solution.py:89
  20.1 0.7 copy.74
  20.8 2.3 %scatter_custom_fusion = s32[480]{0:T(512)S(1)} fusion(s32[256]{0:T(256)S(1)} %bitcast.88, s32[256]{0:T(256)S(1)} %and_select_fusion, s32[]{:T(128)} %constant.72.clone.1), kind=kCustom, calls=%fused_computation.60 | custom fusion | flops 256 | bytes 1924 | tf_op jit(solution)/shard_map/scatter-add | solution.py:60
  23.2 0.0 all-to-all-done.2
  23.2 3.4 %all-to-all-start.1 = ((bf16[64,4,512]{2,0,1:T(8,128)(2,1)}), bf16[64,4,512]{2,0,1:T(8,128)(2,1)S(1)}, u32[]{:S(2)}, u32[]{:S(2)}) async-start(bf16[64,4,512]{2,0,1:T(8,128)(2,1)} %bitcast.71), calls=%async_computation.1 | async-start | bytes 524288 | tf_op jit(solution)/shard_map/all_to_all | solution.py:91
  26.6 5.8 %all-to-all-done.1 = bf16[64,4,512]{2,0,1:T(8,128)(2,1)S(1)} async-done(((bf16[64,4,512]{2,0,1:T(8,128)(2,1)}), bf16[64,4,512]{2,0,1:T(8,128)(2,1)S(1)}, u32[]{:S(2)}, u32[]{:S(2)}) %all-to-all-start.1) | async-done | bytes 262176 | tf_op jit(solution)/shard_map/all_to_all | solution.py:91
  32.4 3.4 %all-to-all-start = ((bf16[64,4,512]{2,0,1:T(8,128)(2,1)}), bf16[64,4,512]{2,0,1:T(8,128)(2,1)S(1)}, u32[]{:S(2)}, u32[]{:S(2)}) async-start(bf16[64,4,512]{2,0,1:T(8,128)(2,1)} %bitcast.72), calls=%async_computation | async-start | bytes 524288 | tf_op jit(solution)/shard_map/all_to_all | solution.py:92
  35.8 0.1 reshape.137
  35.9 0.1 reshape.136
  36.0 5.6 %all-to-all-done = bf16[64,4,512]{2,0,1:T(8,128)(2,1)S(1)} async-done(((bf16[64,4,512]{2,0,1:T(8,128)(2,1)}), bf16[64,4,512]{2,0,1:T(8,128)(2,1)S(1)}, u32[]{:S(2)}, u32[]{:S(2)}) %all-to-all-start) | async-done | bytes 262176 | tf_op jit(solution)/shard_map/all_to_all | solution.py:92
  41.6 0.1 reshape.135
  41.7 0.3 fusion.25
  42.0 0.2 fusion.6
  42.1 0.3 fusion.5
  42.5 0.2 copy.41
  42.7 0.8 all_to_all.72
  43.5 3.4 %all-to-all-start.3 = ((bf16[4,64,512]{2,1,0:T(8,128)(2,1)}), bf16[4,64,512]{2,1,0:T(8,128)(2,1)S(1)}, u32[]{:S(2)}, u32[]{:S(2)}) async-start(bf16[4,64,512]{2,1,0:T(8,128)(2,1)} %all_to_all.72), calls=%async_computation.3 | async-start | bytes 524288 | tf_op jit(solution)/shard_map/all_to_all | solution.py:94
  46.9 0.1 copy.47
  47.0 0.1 reshape.151
  47.1 0.1 broadcast_in_dim.58
  47.2 5.4 %all-to-all-done.3 = bf16[4,64,512]{2,1,0:T(8,128)(2,1)S(1)} async-done(((bf16[4,64,512]{2,1,0:T(8,128)(2,1)}), bf16[4,64,512]{2,1,0:T(8,128)(2,1)S(1)}, u32[]{:S(2)}, u32[]{:S(2)}) %all-to-all-start.3) | async-done | bytes 262176 | tf_op jit(solution)/shard_map/all_to_all | solution.py:94
  52.7 5.0 %fusion = bf16[64,2048]{1,0:T(8,128)(2,1)S(1)} fusion(bf16[64,2048]{1,0:T(8,128)(2,1)S(1)} %bitcast.76, bf16[2048,2048]{1,0:T(8,128)(2,1)} %param.14, bf16[64,2048]{1,0:T(8,128)(2,1)S(1)} %copy-done.2), kind=kOutput, calls=%fused_computation.8 | convolution fusion | flops 537264128 | bytes 9175040 | tf_op jit(solution)/shard_map/dot_general | solution.py:95
  57.7 0.0 copy-done
  57.7 0.2 fusion.27
  57.9 1.9 %gather_fusion.1 = f32[256]{0:T(256)S(1)} fusion(f32[64,60]{1,0:T(8,128)S(1)} %fusion.27, s32[256]{0:T(256)S(1)} %reshape.151), kind=kCustom, calls=%fused_computation.1 | custom fusion | bytes 4096 | tf_op jit(solution)/shard_map/jit(take_along_axis)/gather | solution.py:53
  59.8 0.1 reshape.154
  59.9 0.1 copy.48
  60.0 0.1 copy.49
  60.1 0.1 reshape.169
  60.3 2.5 %scatter_custom_fusion.1 = f32[480]{0:T(512)S(1)} fusion(s32[256]{0:T(256)S(1)} %bitcast.89, f32[256]{0:T(256)S(1)} %reshape.169, f32[]{:T(128)} %constant.70.clone.1), kind=kCustom, calls=%fused_computation.57 | custom fusion | flops 256 | bytes 1924 | tf_op jit(solution)/shard_map/scatter-add | solution.py:61
  62.8 0.1 mul.52
  62.8 2.5 %gather_fusion = bf16[480,2048]{1,0:T(8,128)(2,1)S(1)} fusion(bf16[64,2048]{1,0:T(8,128)(2,1)S(1)} %fusion, s32[1024]{0:T(1024)S(1)} %pad_clamp_fusion), kind=kCustom, calls=%fused_computation | custom fusion | bytes 3934080 | tf_op jit(solution)/shard_map/jit(_take)/gather | solution.py:62
  65.3 1.8 %multiply_convert_fusion = bf16[60,8,2048]{2,1,0:T(8,128)(2,1)} fusion(bf16[480,2048]{1,0:T(8,128)(2,1)S(1)} %gather_fusion, f32[60,8]{1,0:T(8,128)S(1)} %mul.52, pred[60,8]{1,0:T(8,128)(4,1)S(1)} %broadcast_in_dim.58), kind=kLoop, calls=%fused_computation.4 | loop fusion | flops 3932160 | bytes 3934560 | tf_op jit(solution)/shard_map/convert_element_type | solution.py:63
  67.1 3.6 %all-to-all-start.4 = ((bf16[60,8,2048]{2,1,0:T(8,128)(2,1)}), bf16[60,8,2048]{2,1,0:T(8,128)(2,1)S(1)}, u32[]{:S(2)}, u32[]{:S(2)}) async-start(bf16[60,8,2048]{2,1,0:T(8,128)(2,1)} %multiply_convert_fusion), calls=%async_computation.4 | async-start | bytes 3932160 | tf_op jit(solution)/shard_map/all_to_all | solution.py:98
  70.7 0.0 copy-start.1
  70.8 5.0 %fusion.26 = f32[64,2048]{1,0:T(8,128)S(1)} fusion(bf16[64,2048]{1,0:T(8,128)(2,1)S(1)} %fusion, bf16[2048,2048]{1,0:T(8,128)(2,1)} %param.15), kind=kOutput, calls=%fused_computation.64 | convolution fusion | flops 536870912 | bytes 9175040 | tf_op jit(solution)/shard_map/dot_general | solution.py:42
  75.8 9.5 %fusion.2 = bf16[64,2048]{1,0:T(8,128)(2,1)} fusion(bf16[2048,2048]{1,0:T(8,128)(2,1)} %param.17, bf16[64,2048]{1,0:T(8,128)(2,1)S(1)} %fusion, bf16[2048,2048]{1,0:T(8,128)(2,1)} %param.16, f32[64,2048]{1,0:T(8,128)S(1)} %fusion.26), kind=kOutput, calls=%fused_computation.10 | convolution fusion | flops 1074921472 | bytes 17825792 | tf_op jit(solution)/shard_map/dot_general | solution.py:45
  85.3 9.5 %all-to-all-done.4 = bf16[60,8,2048]{2,1,0:T(8,128)(2,1)S(1)} async-done(((bf16[60,8,2048]{2,1,0:T(8,128)(2,1)}), bf16[60,8,2048]{2,1,0:T(8,128)(2,1)S(1)}, u32[]{:S(2)}, u32[]{:S(2)}) %all-to-all-start.4) | async-done | bytes 1966112 | tf_op jit(solution)/shard_map/all_to_all | solution.py:98
  94.8 1.4 %copy.71 = bf16[4,15,8,2048]{3,2,0,1:T(8,128)(2,1)} copy(bf16[4,15,8,2048]{3,2,1,0:T(8,128)(2,1)S(1)} %bitcast.75) | data formatting | bytes 3932160 | tf_op jit(solution)/shard_map/all_to_all | solution.py:98
  96.2 0.0 copy-done.1
  (17 shorter events, 0.2 us)
Async XLA Ops:
  0.6 57.0 %copy-start = (bf16[2048,60]{0,1:T(8,128)(2,1)S(1)}, bf16[2048,60]{0,1:T(8,128)(2,1)}, u32[]{:S(2)}) copy-start(bf16[2048,60]{0,1:T(8,128)(2,1)} %param.18) | copy-start | bytes 737284
  0.6 12.0 %copy-start.2 = (bf16[64,2048]{1,0:T(8,128)(2,1)S(1)}, bf16[64,2048]{1,0:T(8,128)(2,1)}, u32[]{:S(2)}) copy-start(bf16[64,2048]{1,0:T(8,128)(2,1)} %param.10) | copy-start | bytes 786436
  0.7 10.3 %copy-start.3 = (s32[64,4]{0,1:T(4,128)S(1)}, s32[64,4]{0,1:T(4,128)}, u32[]{:S(2)}) copy-start(s32[64,4]{0,1:T(4,128)} %param.19) | copy-start | bytes 3076
  6.5 16.7 %all-to-all-start.2 = ((bf16[64,4,512]{2,0,1:T(8,128)(2,1)}), bf16[64,4,512]{2,0,1:T(8,128)(2,1)S(1)}, u32[]{:S(2)}, u32[]{:S(2)}) async-start(bf16[64,4,512]{2,0,1:T(8,128)(2,1)} %bitcast.70), calls=%async_computation.2 | async-start | bytes 524288 | tf_op jit(solution)/shard_map/all_to_all | solution.py:90
  12.5 6.0 %slice-start = ((s8[8388608]{0:T(1024)(128)(4,1)}), s8[4194304]{0:T(1024)(128)(4,1)S(1)}, s32[]{:S(2)}) async-start(s8[8388608]{0:T(1024)(128)(4,1)} %bitcast.73), calls=%async_computation.5 | async-start | bytes 8388608
  12.6 5.9 %slice-start.1 = ((s8[8388608]{0:T(1024)(128)(4,1)}), s8[4194304]{0:T(1024)(128)(4,1)S(1)}, s32[]{:S(2)}) async-start(s8[8388608]{0:T(1024)(128)(4,1)} %bitcast.73), calls=%async_computation.6 | async-start | bytes 8388608
  23.2 9.2 %all-to-all-start.1 = ((bf16[64,4,512]{2,0,1:T(8,128)(2,1)}), bf16[64,4,512]{2,0,1:T(8,128)(2,1)S(1)}, u32[]{:S(2)}, u32[]{:S(2)}) async-start(bf16[64,4,512]{2,0,1:T(8,128)(2,1)} %bitcast.71), calls=%async_computation.1 | async-start | bytes 524288 | tf_op jit(solution)/shard_map/all_to_all | solution.py:91
  32.4 9.2 %all-to-all-start = ((bf16[64,4,512]{2,0,1:T(8,128)(2,1)}), bf16[64,4,512]{2,0,1:T(8,128)(2,1)S(1)}, u32[]{:S(2)}, u32[]{:S(2)}) async-start(bf16[64,4,512]{2,0,1:T(8,128)(2,1)} %bitcast.72), calls=%async_computation | async-start | bytes 524288 | tf_op jit(solution)/shard_map/all_to_all | solution.py:92
  43.5 9.2 %all-to-all-start.3 = ((bf16[4,64,512]{2,1,0:T(8,128)(2,1)}), bf16[4,64,512]{2,1,0:T(8,128)(2,1)S(1)}, u32[]{:S(2)}, u32[]{:S(2)}) async-start(bf16[4,64,512]{2,1,0:T(8,128)(2,1)} %all_to_all.72), calls=%async_computation.3 | async-start | bytes 524288 | tf_op jit(solution)/shard_map/all_to_all | solution.py:94
  67.1 27.6 %all-to-all-start.4 = ((bf16[60,8,2048]{2,1,0:T(8,128)(2,1)}), bf16[60,8,2048]{2,1,0:T(8,128)(2,1)S(1)}, u32[]{:S(2)}, u32[]{:S(2)}) async-start(bf16[60,8,2048]{2,1,0:T(8,128)(2,1)} %multiply_convert_fusion), calls=%async_computation.4 | async-start | bytes 3932160 | tf_op jit(solution)/shard_map/all_to_all | solution.py:98
  70.7 25.4 %copy-start.1 = (bf16[2048,60]{0,1:T(8,128)(2,1)S(1)}, bf16[2048,60]{0,1:T(8,128)(2,1)}, u32[]{:S(2)}) copy-start(bf16[2048,60]{0,1:T(8,128)(2,1)} %param.18) | copy-start | bytes 737284
where the time goes:
time: 96.7 us; the launch traced here: 96.2 us
  matrix products  32.1 us (33%)
  waiting for transfers between devices  26.3 us (27%)
  starting transfers between devices  18.3 us (19%)
  local copies, waits for them, and re-layouts  10.8 us (11%)
  other arithmetic  7.62 us (8%)
  between operations  0.97 us (1%)
    dot_general x1, matrix products, shared_expert(): jnp.dot(swiglu, w_down, preferred_element_type=jnp.float32)  9.52 us
    all_to_all x1, waiting for transfers between devices, local_step(): expert_buf = lax.all_to_all(send_buf, 'sp', 0, 1, tiled=True)  9.49 us
    all_to_all x1, waiting for transfers between devices, local_step(): lax.all_to_all(head_columns(keys_loc, kv_heads, n_grp), 'sp', 1, 0, tiled...  5.78 us
    all_to_all x1, waiting for transfers between devices, local_step(): lax.all_to_all(head_columns(values_loc, kv_heads, n_grp), 'sp', 1, 0, til...  5.61 us
    all_to_all x1, waiting for transfers between devices, local_step(): attn_loc = lax.all_to_all(attn_heads, 'sp', 0, 1, tiled=True)  5.42 us
    dot_general x1, matrix products, local_step(): jnp.dot(tokens, w_query, preferred_element_type=jnp.float32)  5.1 us
    dot_general x1, matrix products, local_step(): jnp.dot(tokens, w_key, preferred_element_type=jnp.float32)  5.1 us
    dot_general x1, matrix products, shared_expert(): gate_act = jnp.dot(hidden, w_gate, preferred_element_type=jnp.float32)  4.99 us
  transfers between devices with their start and end apart: 5, of which 4 were waited for; matrix products, arithmetic and copies ran while one was open for 28% of the time, Pallas kernels for 0%

commit v1 on v0

v1 whole, which is shorter than its diff:
```python
import math
import jax
import jax.numpy as jnp
from jax import lax
from jax.experimental import pallas as pl
from jax.experimental.pallas import tpu as pltpu
from jax.sharding import PartitionSpec as P

MESH = pl.DeviceIdType.MESH
F32 = jnp.float32
BF16 = jnp.bfloat16

HD = 128
D = 2048
HALF = 1024
TOK = 64
CHIP = 128
SEQ = 256
NX = 8
XC = D // NX
NEXP = 15
CAP = 8
SLOTS = 32


def dot(a, b):
    return jnp.dot(a, b, preferred_element_type=F32)


def dot_t(a, b):
    return lax.dot_general(a, b, (((1,), (1,)), ((), ())), preferred_element_type=F32)


def body(x_ref, wq, wk, wv, wo, wg, wu, wd, wr, ids_ref, y_ref, buf_ref,
         x_v, w_v, wo_v, wg_v, wu_v, wd_v, wr_v, ids_v,
         qkv_v, acc_v, o_own, o_oth, hacc_v, h_own, h_oth, ga_v, ua_v, a_own, a_oth, ya_v, y_v,
         wmap_v, p_v, lt_v, gate_v, st_v,
         s_x, s_w, s_w2, s_misc, s_out,
         xi_s, xi_r, xr_s, xr_r, xp_s, xp_r, id_s, id_r, o_s, o_r, h_s, h_r, a_s, a_r):
    dp = lax.axis_index("dp")
    s = lax.axis_index("sp")
    chip = s // 2
    j = s % 2
    partner = chip * 2 + (1 - j)
    remote = (1 - chip) * 2 + j
    diag = (1 - chip) * 2 + (1 - j)
    jo = pl.multiple_of(j * HALF, HALF)
    jn = pl.multiple_of((1 - j) * HALF, HALF)
    r_own = pl.ds(pl.multiple_of(s * TOK, TOK), TOK)
    r_remote = pl.ds(pl.multiple_of(remote * TOK, TOK), TOK)
    r_L = pl.ds(pl.multiple_of(chip * CHIP, CHIP), CHIP)
    r_R = pl.ds(pl.multiple_of((1 - chip) * CHIP, CHIP), CHIP)

    barrier = pltpu.get_barrier_semaphore()
    for p in (partner, remote, diag):
        pl.semaphore_signal(barrier, inc=1, device_id=(dp, p), device_id_type=MESH)

    x_in = pltpu.make_async_copy(x_ref, x_v.at[r_own, :], s_x.at[0])
    x_in.start()
    ids_in = pltpu.make_async_copy(ids_ref, ids_v.at[s], s_x.at[1])
    ids_in.start()
    loads = []
    for i, w in enumerate((wk, wv, wq)):
        for n in range(2):
            c = pltpu.make_async_copy(
                w.at[:, pl.ds(pl.multiple_of(j * HALF + n * 512, 512), 512)],
                w_v.at[i, :, pl.ds(n * 512, 512)], s_w.at[i * 2 + n])
            c.start()
            loads.append(c)
    loads2 = []
    for i, (w, v) in enumerate(((wo, wo_v), (wg, wg_v), (wu, wu_v))):
        for n, off in enumerate((jo, jn)):
            c = pltpu.make_async_copy(w.at[pl.ds(off, HALF), pl.ds(jo, HALF)], v.at[n], s_w2.at[i * 2 + n])
            c.start()
            loads2.append(c)
    for n, off in enumerate((jo, jn)):
        for m, coff in enumerate((jo, jn)):
            c = pltpu.make_async_copy(wd.at[pl.ds(off, HALF), pl.ds(coff, HALF)],
                                      wd_v.at[n, :, pl.ds(m * HALF, HALF)], s_w2.at[6 + n * 2 + m])
            c.start()
            loads2.append(c)
    wr_in = [pltpu.make_async_copy(wr.at[:, pl.ds(off, HALF)], wr_v.at[n], s_misc.at[n]) for n, off in enumerate((jo, jn))]
    for c in wr_in:
        c.start()

    def rcopy(src, dst, ss, rs, p):
        return pltpu.make_async_remote_copy(src_ref=src, dst_ref=dst, send_sem=ss, recv_sem=rs,
                                            device_id=(dp, p), device_id_type=MESH)

    def x_ici(k):
        c = pl.ds(pl.multiple_of(k * XC, XC), XC)
        return rcopy(x_v.at[r_own, c], x_v.at[r_own, c], xi_s.at[k], xi_r.at[k], remote)

    def x_relay(k):
        c = pl.ds(pl.multiple_of(k * XC, XC), XC)
        return rcopy(x_v.at[r_remote, c], x_v.at[r_remote, c], xr_s.at[k], xr_r.at[k], partner)

    pl.semaphore_wait(barrier, 3)
    x_in.wait()
    ids_in.wait()
    x_part = rcopy(x_v.at[r_own, :], x_v.at[r_own, :], xp_s.at[0], xp_r.at[0], partner)
    x_part.start()
    for k in range(NX):
        x_ici(k).start()
    id_copies = [rcopy(ids_v.at[s], ids_v.at[s], id_s.at[n], id_r.at[n], p) for n, p in enumerate((partner, remote, diag))]
    for c in id_copies:
        c.start()

    x_part.wait_recv()
    for i in range(3):
        for n in range(2):
            loads[i * 2 + n].wait()
            qkv_v[i, r_L, n * 512:(n + 1) * 512] = dot(x_v[r_L, :], w_v[i, :, n * 512:(n + 1) * 512]).astype(BF16)

    for c in id_copies:
        c.wait_recv()
    idst = jnp.concatenate([ids_v[t] for t in range(4)], axis=1)
    e_ids = lax.broadcasted_iota(jnp.int32, (16, SEQ), 0) + NEXP * s
    hit = jnp.zeros((16, SEQ), F32)
    for c in range(4):
        hit = jnp.where(idst[c:c + 1, :] == e_ids, 1.0, hit)
    t_row = lax.broadcasted_iota(jnp.int32, (SEQ, SEQ), 0)
    t_col = lax.broadcasted_iota(jnp.int32, (SEQ, SEQ), 1)
    earlier = jnp.where((t_row < t_col) & (t_row // TOK == t_col // TOK), 1.0, 0.0).astype(BF16)
    rank = dot(hit.astype(BF16), earlier)
    src8 = (CAP * (lax.broadcasted_iota(jnp.int32, (16, SEQ), 1) // TOK)).astype(F32)
    wmap = jnp.where((hit > 0.5) & (rank < CAP - 0.5), rank + src8, 99.0)
    wmap_v[...] = wmap
    slot = lax.broadcasted_iota(jnp.int32, (SLOTS, SEQ), 0).astype(F32)
    for e in range(NEXP):
        p_v[e * SLOTS:(e + 1) * SLOTS, :] = jnp.where(wmap[e:e + 1, :] == slot, 1.0, 0.0).astype(BF16)

    acc_v[...] = jnp.zeros_like(acc_v)
    x_ici(0).wait_recv()
    x_relay(0).start()

    def r_step(k, carry):
        x_ici(k + 1).wait_recv()
        x_relay(k + 1).start()
        x_relay(k).wait_recv()
        c = pl.ds(pl.multiple_of(k * XC, XC), XC)
        xr = x_v[r_R, c]
        for i in range(3):
            acc_v[i] += dot(xr, w_v[i, c, :])
        return carry

    lax.fori_loop(0, NX - 1, r_step, 0)
    x_relay(NX - 1).wait_recv()
    xr = x_v[r_R, D - XC:]
    for i in range(3):
        qkv_v[i, r_R, :] = (acc_v[i] + dot(xr, w_v[i, D - XC:, :])).astype(BF16)

    scale = 1.0 / math.sqrt(HD)
    tri = lax.broadcasted_iota(jnp.int32, (CHIP, CHIP), 0) >= lax.broadcasted_iota(jnp.int32, (CHIP, CHIP), 1)
    o_copies = []
    for hd in range(8):
        c = slice(hd * HD, (hd + 1) * HD)
        k_h, v_h, q_h = qkv_v[0, :, c], qkv_v[1, :, c], qkv_v[2, :, c]
        sc = dot_t(q_h, k_h) * scale
        top = jnp.where(tri, sc[:CHIP, :CHIP], -jnp.inf)
        bot0 = sc[CHIP:, :CHIP]
        bot1 = jnp.where(tri, sc[CHIP:, CHIP:], -jnp.inf)
        e_top = jnp.exp(top - jnp.max(top, axis=1, keepdims=True))
        p_top = (e_top * (1.0 / jnp.sum(e_top, axis=1, keepdims=True))).astype(BF16)
        m_bot = jnp.max(jnp.maximum(bot0, bot1), axis=1, keepdims=True)
        e0, e1 = jnp.exp(bot0 - m_bot), jnp.exp(bot1 - m_bot)
        inv = 1.0 / jnp.sum(e0 + e1, axis=1, keepdims=True)
        p_bot = jnp.concatenate([(e0 * inv).astype(BF16), (e1 * inv).astype(BF16)], axis=1)
        o_own[:CHIP, c] = dot(p_top, v_h[:CHIP]).astype(BF16)
        o_own[CHIP:, c] = dot(p_bot, v_h).astype(BF16)
        if hd % 2 == 1:
            n = hd // 2
            cc = slice(n * 256, (n + 1) * 256)
            cp = rcopy(o_own.at[:, cc], o_oth.at[:, cc], o_s.at[n], o_r.at[n], partner)
            cp.start()
            o_copies.append(cp)

    loads2[0].wait()
    loads2[1].wait()
    hacc_v[...] = dot(o_own[...], wo_v[0])
    for cp in o_copies:
        cp.wait_recv()
    h_copies = []
    for n in range(4):
        cc = slice(n * 256, (n + 1) * 256)
        xc = x_v[:, pl.ds(pl.multiple_of(j * HALF + n * 256, 256), 256)].astype(F32)
        h_own[:, cc] = (xc + (hacc_v[:, cc] + dot(o_oth[...], wo_v[1, :, cc]))).astype(BF16)
        cp = rcopy(h_own.at[:, cc], h_oth.at[:, cc], h_s.at[n], h_r.at[n], partner)
        cp.start()
        h_copies.append(cp)

    for c in loads2[2:6]:
        c.wait()
    ga_v[...] = dot(h_own[r_L, :], wg_v[0])
    ua_v[...] = dot(h_own[r_L, :], wu_v[0])
    for cp in h_copies:
        cp.wait_recv()
    a_copies = []
    r_mine = pl.ds(pl.multiple_of(j * TOK, TOK), TOK)
    r_his = pl.ds(pl.multiple_of((1 - j) * TOK, TOK), TOK)
    for n in range(4):
        cc = slice(n * 256, (n + 1) * 256)
        g = ga_v[:, cc] + dot(h_oth[r_L, :], wg_v[1, :, cc])
        u = ua_v[:, cc] + dot(h_oth[r_L, :], wu_v[1, :, cc])
        a_own[:, cc] = (jax.nn.silu(g) * u).astype(BF16)
        cp = rcopy(a_own.at[r_his, cc], a_oth.at[:, cc], a_s.at[n], a_r.at[n], partner)
        cp.start()
        a_copies.append(cp)

    for c in wr_in:
        c.wait()
    logits = dot_t(h_own[...], wr_v[0]) + dot_t(h_oth[...], wr_v[1])
    lt_v[...] = jax.nn.sigmoid(logits.T)
    for e in range(NEXP):
        g_row = lt_v[pl.ds(NEXP * s + e, 1), :]
        picked = jnp.where(wmap_v[e:e + 1, :] == slot, g_row, 0.0)
        gate_v[e * SLOTS:(e + 1) * SLOTS, :] = jnp.broadcast_to(jnp.sum(picked, axis=1, keepdims=True), (SLOTS, HD))
    outs = []
    for m, (h, off) in enumerate(((h_own, jo), (h_oth, jn))):
        for n in range(4):
            cc = slice(n * 256, (n + 1) * 256)
            rows = dot(p_v[...], h[:, cc])
            gate = gate_v[...]
            st_v[m, :, cc] = (rows * jnp.concatenate([gate, gate], axis=1)).astype(BF16)
        cp = pltpu.make_async_copy(st_v.at[m], buf_ref.at[:, pl.ds(off, HALF)], s_out.at[m])
        cp.start()
        outs.append(cp)

    for c in loads2[6:]:
        c.wait()
    ya_v[...] = dot(a_own[r_mine, :], wd_v[0])
    for cp in a_copies:
        cp.wait_recv()
    for m, (h, off) in enumerate(((h_own, jo), (h_oth, jn))):
        cc = slice(m * HALF, (m + 1) * HALF)
        part = ya_v[:, cc] + dot(a_oth[...], wd_v[1, :, cc])
        y_v[:, cc] = (h[r_own, :].astype(F32) + part).astype(BF16)
        cp = pltpu.make_async_copy(y_v.at[:, cc], y_ref.at[:, pl.ds(off, HALF)], s_out.at[2 + m])
        cp.start()
        outs.append(cp)

    x_part.wait_send()
    for k in range(NX):
        x_ici(k).wait_send()
        x_relay(k).wait_send()
    for cp in id_copies + o_copies + h_copies + a_copies:
        cp.wait_send()
    for cp in outs:
        cp.wait()


def fused(x, wq, wk, wv, wo, wg, wu, wd, wr, ids):
    hbm = pl.BlockSpec(memory_space=pltpu.HBM)
    v = pltpu.VMEM
    dma = pltpu.SemaphoreType.DMA
    return pl.pallas_call(
        body,
        out_shape=(jax.ShapeDtypeStruct((TOK, D), BF16), jax.ShapeDtypeStruct((NEXP * SLOTS, D), BF16)),
        in_specs=[hbm] * 10,
        out_specs=(hbm, hbm),
        scratch_shapes=[
            v((SEQ, D), BF16), v((3, D, HALF), BF16), v((2, HALF, HALF), BF16), v((2, HALF, HALF), BF16),
            v((2, HALF, HALF), BF16), v((2, HALF, D), BF16), v((2, 60, HALF), BF16), v((4, 4, TOK), jnp.int32),
            v((3, SEQ, HALF), BF16), v((3, CHIP, HALF), F32), v((SEQ, HALF), BF16), v((SEQ, HALF), BF16),
            v((SEQ, HALF), F32), v((SEQ, HALF), BF16), v((SEQ, HALF), BF16), v((CHIP, HALF), F32),
            v((CHIP, HALF), F32), v((CHIP, HALF), BF16), v((TOK, HALF), BF16), v((TOK, D), F32), v((TOK, D), BF16),
            v((16, SEQ), F32), v((NEXP * SLOTS, SEQ), BF16), v((60, SEQ), F32), v((NEXP * SLOTS, HD), F32),
            v((2, NEXP * SLOTS, HALF), BF16),
            dma((2,)), dma((6,)), dma((10,)), dma((2,)), dma((4,)),
            dma((NX,)), dma((NX,)), dma((NX,)), dma((NX,)), dma((1,)), dma((1,)), dma((3,)), dma((3,)),
            dma((4,)), dma((4,)), dma((4,)), dma((4,)), dma((4,)), dma((4,)),
        ],
        compiler_params=pltpu.CompilerParams(collective_id=0, has_side_effects=True,
                                             vmem_limit_bytes=60 * 1024 * 1024),
        cost_estimate=pl.CostEstimate(flops=6_000_000_000, bytes_accessed=36_000_000, transcendentals=600_000),
        name="fused_block",
    )(x, wq, wk, wv, wo, wg, wu, wd, wr, ids)


def solution(mesh):
    row_spec = P(('dp', 'sp'), None)
    buf_spec = P(('dp', 'sp'), None, None)
    replicated = P()

    def local_step(tokens, w_query, w_key, w_value, w_out, w_gate, w_up, w_down, w_router, expert_ids):
        y, buf = fused(tokens, w_query, w_key, w_value, w_out, w_gate, w_up, w_down, w_router.T, expert_ids.T)
        return y, buf.reshape(NEXP, SLOTS, D)

    return jax.shard_map(local_step, mesh=mesh, in_specs=(row_spec,) + (replicated,) * 8 + (row_spec,),
                         out_specs=(row_spec, buf_spec), check_vma=False)
```

time: 96.7 us -> 44.5 us (0.46)
  Pallas kernels: 0 us -> 39 us
  matrix products: 32.1 us -> 0 us
  waiting for transfers between devices: 26.3 us -> 0 us
  starting transfers between devices: 18.3 us -> 0 us
  other arithmetic: 7.62 us -> 0 us
  local copies, waits for them, and re-layouts: 10.8 us -> 4.71 us
    pallas_call x0 -> x1, Pallas kernels: none -> 39 us  [fused(): pl.pallas_call(body, out_shape=(jax.ShapeDtypeStruct((TOK, D), BF16), jax...]
    dot_general x9 -> x0, matrix products: 32.1 us -> none  [the longest x1 9.52 us: shared_expert(): jnp.dot(swiglu, w_down, preferred_element_type=jnp.float32)]
    all_to_all x5 -> x0, waiting for transfers between devices: 26.3 us -> none  [the longest x1 9.49 us: local_step(): expert_buf = lax.all_to_all(send_buf, 'sp', 0, 1, tiled=True)]
    all_to_all x5 -> x0, starting transfers between devices: 18.3 us -> none  [the longest x1 4.5 us: local_step(): q_all = lax.all_to_all(queries, 'sp', 1, 0, tiled=True)]
    scatter-add x2 -> x0, other arithmetic: 4.81 us -> none  [the longest x1 2.49 us: dispatch_rows(): slot_gate = jax.ops.segment_sum(gate_vals, dest_row, num_segments=n_slots)]
    gather x6 -> x0, local copies, waits for them, and re-layouts: 4.81 us -> none  [the longest x1 2.49 us: dispatch_rows(): gathered = jnp.take(hidden, slot_token, axis=0)]
    unnamed x15 -> x2, local copies, waits for them, and re-layouts: 0.17 us -> 4.71 us
    all_to_all x6 -> x0, local copies, waits for them, and re-layouts: 4.39 us -> none  [the longest x1 1.4 us: local_step(): expert_buf = lax.all_to_all(send_buf, 'sp', 0, 1, tiled=True)]
  transfers between devices with their start and end apart: 5 -> 0, of which waited for: 4 -> 0; matrix products, arithmetic and copies ran while one was open for 28% -> 0% of each run, Pallas kernels for 0% -> 0%
where the time goes in v1:
time: 44.5 us; the launch traced here: 44.4 us
  Pallas kernels  39 us (88%)
  local copies, waits for them, and re-layouts  4.71 us (11%)
  between operations  0.64 us (1%)
    pallas_call x1, Pallas kernels, fused(): pl.pallas_call(body, out_shape=(jax.ShapeDtypeStruct((TOK, D), BF16), jax...  39 us
    unnamed x2, local copies, waits for them, and re-layouts  4.71 us

profile of v1, /device:TPU:0, one launch (start us, length us, event | category | flops | bytes accessed | tf_op | source)
XLA Modules:
  0.0 44.4 jit_solution(13820338345696394942)
XLA Ops:
  0.6 39.0 %fused_block.1 = (bf16[64,2048]{1,0:T(8,128)(2,1)}, bf16[480,2048]{1,0:T(8,128)(2,1)}) custom-call(bf16[64,2048]{1,0:T(8,128)(2,1)} %x_ref.1, bf16[2048,2048]{1,0:T(8,128)(2,1)} %wq.1, bf16[2048,2048]{1,0:T(8,128)(2,1)} %wk.1, bf16[2048,2048]{1,0:T(8,128)(2,1)} %wv.1, bf16[2048,2048]{1,0:T(8,128)(2,1)} %wo.1, bf16[2048,2048]{1,0:T(8,128)(2,1)} %wg.1, ...), custom_call_target="tpu_custom_call" | custom-call | flops 6000000000 | bytes 36000000 | tf_op jit(solution)/shard_map/fused_block/pallas_call | solution.py:256
  39.7 1.7 %copy.14 = bf16[64,2048]{1,0:T(8,128)(2,1)} copy(bf16[64,2048]{1,0:T(8,128)(2,1)} %get-tuple-element.8) | data formatting | bytes 524288
  41.3 3.0 %copy.15 = bf16[15,32,2048]{2,1,0:T(8,128)(2,1)} copy(bf16[15,32,2048]{2,1,0:T(8,128)(2,1)} %bitcast.3) | data formatting | bytes 3932160

commit v2 on v1

v2 whole, which is shorter than its diff:
```python
import math
import jax
import jax.numpy as jnp
from jax import lax
from jax.experimental import pallas as pl
from jax.experimental.pallas import tpu as pltpu
from jax.sharding import PartitionSpec as P

MESH = pl.DeviceIdType.MESH
F32 = jnp.float32
BF16 = jnp.bfloat16

HD = 128
D = 2048
HALF = 1024
TOK = 64
CHIP = 128
SEQ = 256
NX = 8
XC = D // NX
NEXP = 15
CAP = 8
SLOTS = 32


def dot(a, b):
    return jnp.dot(a, b, preferred_element_type=F32)


def dot_t(a, b):
    return lax.dot_general(a, b, (((1,), (1,)), ((), ())), preferred_element_type=F32)


def body(x_ref, wq, wk, wv, wo, wg, wu, wd, wr, ids_ref, y_ref, buf_ref,
         x_v, w_v, wo_v, wg_v, wu_v, wd_v, wr_v, ids_v,
         qkv_v, acc_v, o_own, o_oth, hacc_v, h_own, h_oth, ga_v, ua_v, a_own, a_oth, ya_v,
         wmap_v, p_v, lt_v, gate_v,
         s_x, s_w, s_w2, s_misc,
         xi_s, xi_r, xr_s, xr_r, xp_s, xp_r, id_s, id_r, o_s, o_r, h_s, h_r, a_s, a_r):
    dp = lax.axis_index("dp")
    s = lax.axis_index("sp")
    chip = s // 2
    j = s % 2
    partner = chip * 2 + (1 - j)
    remote = (1 - chip) * 2 + j
    diag = (1 - chip) * 2 + (1 - j)
    jo = pl.multiple_of(j * HALF, HALF)
    jn = pl.multiple_of((1 - j) * HALF, HALF)
    r_own = pl.ds(pl.multiple_of(s * TOK, TOK), TOK)
    r_remote = pl.ds(pl.multiple_of(remote * TOK, TOK), TOK)
    r_L = pl.ds(pl.multiple_of(chip * CHIP, CHIP), CHIP)
    r_R = pl.ds(pl.multiple_of((1 - chip) * CHIP, CHIP), CHIP)

    barrier = pltpu.get_barrier_semaphore()
    for p in (partner, remote, diag):
        pl.semaphore_signal(barrier, inc=1, device_id=(dp, p), device_id_type=MESH)

    def rcopy(src, dst, ss, rs, p):
        return pltpu.make_async_remote_copy(src_ref=src, dst_ref=dst, send_sem=ss, recv_sem=rs,
                                            device_id=(dp, p), device_id_type=MESH)

    def x_ici(k):
        c = pl.ds(pl.multiple_of(k * XC, XC), XC)
        return rcopy(x_v.at[r_own, c], x_v.at[r_own, c], xi_s.at[k], xi_r.at[k], remote)

    def x_relay(k):
        c = pl.ds(pl.multiple_of(k * XC, XC), XC)
        return rcopy(x_v.at[r_remote, c], x_v.at[r_remote, c], xr_s.at[k], xr_r.at[k], partner)

    x_in = pltpu.make_async_copy(x_ref, x_v.at[r_own, :], s_x.at[0])
    x_in.start()
    ids_in = pltpu.make_async_copy(ids_ref, ids_v.at[s], s_x.at[1])
    ids_in.start()
    x_in.wait()
    ids_in.wait()
    pl.semaphore_wait(barrier, 3)
    id_copies = [rcopy(ids_v.at[s], ids_v.at[s], id_s.at[n], id_r.at[n], p) for n, p in enumerate((partner, remote, diag))]
    for c in id_copies:
        c.start()
    x_part = rcopy(x_v.at[r_own, :], x_v.at[r_own, :], xp_s.at[0], xp_r.at[0], partner)
    x_part.start()
    for k in range(NX):
        x_ici(k).start()

    loads = []
    for i, w in enumerate((wk, wv, wq)):
        for n in range(2):
            c = pltpu.make_async_copy(
                w.at[:, pl.ds(pl.multiple_of(j * HALF + n * 512, 512), 512)],
                w_v.at[i, :, pl.ds(n * 512, 512)], s_w.at[i * 2 + n])
            c.start()
            loads.append(c)
    loads2 = []
    for i, (w, v) in enumerate(((wo, wo_v), (wg, wg_v), (wu, wu_v))):
        for n, off in enumerate((jo, jn)):
            loads2.append(pltpu.make_async_copy(w.at[pl.ds(off, HALF), pl.ds(jo, HALF)], v.at[n], s_w2.at[i * 2 + n]))
    for n, off in enumerate((jo, jn)):
        for m, coff in enumerate((jo, jn)):
            loads2.append(pltpu.make_async_copy(wd.at[pl.ds(off, HALF), pl.ds(coff, HALF)],
                                                wd_v.at[n, :, pl.ds(m * HALF, HALF)], s_w2.at[6 + n * 2 + m]))
    wr_in = [pltpu.make_async_copy(wr.at[:, pl.ds(off, HALF)], wr_v.at[n], s_misc.at[n]) for n, off in enumerate((jo, jn))]

    x_part.wait_recv()
    for i in range(3):
        for n in range(2):
            loads[i * 2 + n].wait()
            qkv_v[i, r_L, n * 512:(n + 1) * 512] = dot(x_v[r_L, :], w_v[i, :, n * 512:(n + 1) * 512]).astype(BF16)
            k = i * 2 + n - 2
            if k >= 0:
                x_ici(k).wait_recv()
                x_relay(k).start()
    for c in loads2[:2] + wr_in + loads2[2:]:
        c.start()

    for c in id_copies:
        c.wait_recv()
    idst = jnp.concatenate([ids_v[t] for t in range(4)], axis=1)
    e_ids = lax.broadcasted_iota(jnp.int32, (16, SEQ), 0) + NEXP * s
    hit = jnp.zeros((16, SEQ), F32)
    for c in range(4):
        hit = jnp.where(idst[c:c + 1, :] == e_ids, 1.0, hit)
    t_row = lax.broadcasted_iota(jnp.int32, (SEQ, SEQ), 0)
    t_col = lax.broadcasted_iota(jnp.int32, (SEQ, SEQ), 1)
    earlier = jnp.where((t_row < t_col) & (t_row // TOK == t_col // TOK), 1.0, 0.0).astype(BF16)
    rank = dot(hit.astype(BF16), earlier)
    src8 = (CAP * (lax.broadcasted_iota(jnp.int32, (16, SEQ), 1) // TOK)).astype(F32)
    wmap = jnp.where((hit > 0.5) & (rank < CAP - 0.5), rank + src8, 99.0)
    wmap_v[...] = wmap
    slot = lax.broadcasted_iota(jnp.int32, (SLOTS, SEQ), 0).astype(F32)
    for e in range(NEXP):
        p_v[e * SLOTS:(e + 1) * SLOTS, :] = jnp.where(wmap[e:e + 1, :] == slot, 1.0, 0.0).astype(BF16)

    for k in range(NX):
        if k + 2 >= 4 and k + 2 < NX:
            x_ici(k + 2).wait_recv()
            x_relay(k + 2).start()
        x_relay(k).wait_recv()
        c = slice(k * XC, (k + 1) * XC)
        xr = x_v[r_R, c]
        for i in range(3):
            part = dot(xr, w_v[i, c, :])
            if k == 0:
                acc_v[i] = part
            elif k < NX - 1:
                acc_v[i] += part
            else:
                qkv_v[i, r_R, :] = (acc_v[i] + part).astype(BF16)

    scale = 1.0 / math.sqrt(HD)
    tri = lax.broadcasted_iota(jnp.int32, (CHIP, CHIP), 0) >= lax.broadcasted_iota(jnp.int32, (CHIP, CHIP), 1)
    def scores(hd):
        c = slice(hd * HD, (hd + 1) * HD)
        return dot_t(qkv_v[2, :, c], qkv_v[0, :, c])

    def probs(sc):
        sc = sc * scale
        top = jnp.where(tri, sc[:CHIP, :CHIP], -jnp.inf)
        bot0 = sc[CHIP:, :CHIP]
        bot1 = jnp.where(tri, sc[CHIP:, CHIP:], -jnp.inf)
        e_top = jnp.exp(top - jnp.max(top, axis=1, keepdims=True))
        p_top = (e_top * (1.0 / jnp.sum(e_top, axis=1, keepdims=True))).astype(BF16)
        m_bot = jnp.max(jnp.maximum(bot0, bot1), axis=1, keepdims=True)
        e0, e1 = jnp.exp(bot0 - m_bot), jnp.exp(bot1 - m_bot)
        inv = 1.0 / jnp.sum(e0 + e1, axis=1, keepdims=True)
        return p_top, jnp.concatenate([(e0 * inv).astype(BF16), (e1 * inv).astype(BF16)], axis=1)

    def weighted(hd, p):
        c = slice(hd * HD, (hd + 1) * HD)
        v_h = qkv_v[1, :, c]
        o_own[:CHIP, c] = dot(p[0], v_h[:CHIP]).astype(BF16)
        o_own[CHIP:, c] = dot(p[1], v_h).astype(BF16)

    o_copies = []
    for n in range(2):
        heads = range(n * 4, n * 4 + 4)
        sc = [scores(hd) for hd in heads]
        pr = [probs(t) for t in sc]
        for hd, p in zip(heads, pr):
            weighted(hd, p)
        cc = slice(n * 512, (n + 1) * 512)
        cp = rcopy(o_own.at[:, cc], o_oth.at[:, cc], o_s.at[n], o_r.at[n], partner)
        cp.start()
        o_copies.append(cp)

    loads2[0].wait()
    loads2[1].wait()
    hacc_v[...] = dot(o_own[...], wo_v[0])
    for cp in o_copies:
        cp.wait_recv()
    h_copies = []
    for n in range(2):
        cc = slice(n * 512, (n + 1) * 512)
        xc = x_v[:, pl.ds(pl.multiple_of(j * HALF + n * 512, 512), 512)].astype(F32)
        h_own[:, cc] = (xc + (hacc_v[:, cc] + dot(o_oth[...], wo_v[1, :, cc]))).astype(BF16)
        cp = rcopy(h_own.at[:, cc], h_oth.at[:, cc], h_s.at[n], h_r.at[n], partner)
        cp.start()
        h_copies.append(cp)

    for c in loads2[2:6]:
        c.wait()
    ga_v[...] = dot(h_own[r_L, :], wg_v[0])
    ua_v[...] = dot(h_own[r_L, :], wu_v[0])
    for cp in h_copies:
        cp.wait_recv()
    a_copies = []
    r_mine = pl.ds(pl.multiple_of(j * TOK, TOK), TOK)
    r_his = pl.ds(pl.multiple_of((1 - j) * TOK, TOK), TOK)
    for n in range(2):
        cc = slice(n * 512, (n + 1) * 512)
        g = ga_v[:, cc] + dot(h_oth[r_L, :], wg_v[1, :, cc])
        u = ua_v[:, cc] + dot(h_oth[r_L, :], wu_v[1, :, cc])
        a_own[:, cc] = (jax.nn.silu(g) * u).astype(BF16)
        cp = rcopy(a_own.at[r_his, cc], a_oth.at[:, cc], a_s.at[n], a_r.at[n], partner)
        cp.start()
        a_copies.append(cp)

    for c in wr_in:
        c.wait()
    logits = dot_t(h_own[...], wr_v[0]) + dot_t(h_oth[...], wr_v[1])
    lt_v[...] = jax.nn.sigmoid(logits.T)
    for e in range(NEXP):
        g_row = lt_v[pl.ds(NEXP * s + e, 1), :]
        picked = jnp.where(wmap_v[e:e + 1, :] == slot, g_row, 0.0)
        gate_v[e * SLOTS:(e + 1) * SLOTS, :] = jnp.broadcast_to(jnp.sum(picked, axis=1, keepdims=True), (SLOTS, HD))
    for h, first in ((h_own, j), (h_oth, 1 - j)):
        for n in range(4):
            rows = dot(p_v[...], h[:, n * 256:(n + 1) * 256])
            gate = gate_v[...]
            buf_ref[:, pl.ds(pl.multiple_of(first * HALF + n * 256, 256), 256)] = (
                rows * jnp.concatenate([gate, gate], axis=1)).astype(BF16)

    for c in loads2[6:]:
        c.wait()
    ya_v[...] = dot(a_own[r_mine, :], wd_v[0])
    for cp in a_copies:
        cp.wait_recv()
    for m, (h, off) in enumerate(((h_own, jo), (h_oth, jn))):
        cc = slice(m * HALF, (m + 1) * HALF)
        part = ya_v[:, cc] + dot(a_oth[...], wd_v[1, :, cc])
        y_ref[:, pl.ds(off, HALF)] = (h[r_own, :].astype(F32) + part).astype(BF16)

    x_part.wait_send()
    for k in range(NX):
        x_ici(k).wait_send()
        x_relay(k).wait_send()
    for cp in id_copies + o_copies + h_copies + a_copies:
        cp.wait_send()


def fused(x, wq, wk, wv, wo, wg, wu, wd, wr, ids):
    hbm = pl.BlockSpec(memory_space=pltpu.HBM)
    v = pltpu.VMEM
    dma = pltpu.SemaphoreType.DMA
    return pl.pallas_call(
        body,
        out_shape=(v((TOK, D), BF16), v((NEXP * SLOTS, D), BF16)),
        in_specs=[hbm] * 10,
        out_specs=(pl.BlockSpec(memory_space=v),) * 2,
        scratch_shapes=[
            v((SEQ, D), BF16), v((3, D, HALF), BF16), v((2, HALF, HALF), BF16), v((2, HALF, HALF), BF16),
            v((2, HALF, HALF), BF16), v((2, HALF, D), BF16), v((2, 60, HALF), BF16), v((4, 4, TOK), jnp.int32),
            v((3, SEQ, HALF), BF16), v((3, CHIP, HALF), F32), v((SEQ, HALF), BF16), v((SEQ, HALF), BF16),
            v((SEQ, HALF), F32), v((SEQ, HALF), BF16), v((SEQ, HALF), BF16), v((CHIP, HALF), F32),
            v((CHIP, HALF), F32), v((CHIP, HALF), BF16), v((TOK, HALF), BF16), v((TOK, D), F32),
            v((16, SEQ), F32), v((NEXP * SLOTS, SEQ), BF16), v((60, SEQ), F32), v((NEXP * SLOTS, HD), F32),
            dma((2,)), dma((6,)), dma((10,)), dma((2,)),
            dma((NX,)), dma((NX,)), dma((NX,)), dma((NX,)), dma((1,)), dma((1,)), dma((3,)), dma((3,)),
            dma((2,)), dma((2,)), dma((2,)), dma((2,)), dma((2,)), dma((2,)),
        ],
        compiler_params=pltpu.CompilerParams(collective_id=0, has_side_effects=True,
                                             vmem_limit_bytes=60 * 1024 * 1024),
        cost_estimate=pl.CostEstimate(flops=6_000_000_000, bytes_accessed=36_000_000, transcendentals=600_000),
        name="fused_block",
    )(x, wq, wk, wv, wo, wg, wu, wd, wr, ids)


def solution(mesh):
    row_spec = P(('dp', 'sp'), None)
    buf_spec = P(('dp', 'sp'), None, None)
    replicated = P()

    def local_step(tokens, w_query, w_key, w_value, w_out, w_gate, w_up, w_down, w_router, expert_ids):
        y, buf = fused(tokens, w_query, w_key, w_value, w_out, w_gate, w_up, w_down, w_router.T, expert_ids.T)
        return y, buf.reshape(NEXP, SLOTS, D)

    return jax.shard_map(local_step, mesh=mesh, in_specs=(row_spec,) + (replicated,) * 8 + (row_spec,),
                         out_specs=(row_spec, buf_spec), check_vma=False)
```

time: 44.5 us -> 23.8 us (0.53)
  Pallas kernels: 39 us -> 21 us
  local copies, waits for them, and re-layouts: 4.71 us -> 1.98 us
    pallas_call x1, Pallas kernels: 39 us -> 21 us  [fused(): pl.pallas_call(body, out_shape=(v((TOK, D), BF16), v((NEXP * SLOTS, D), B...]
    unnamed x2, local copies, waits for them, and re-layouts: 4.71 us -> 1.98 us
where the time goes in v2:
time: 23.8 us; the launch traced here: 23.6 us
  Pallas kernels  21 us (88%)
  local copies, waits for them, and re-layouts  1.98 us (8%)
  between operations  0.64 us (3%)
    pallas_call x1, Pallas kernels, fused(): pl.pallas_call(body, out_shape=(v((TOK, D), BF16), v((NEXP * SLOTS, D), B...  21 us
    unnamed x2, local copies, waits for them, and re-layouts  1.98 us

profile of v2, /device:TPU:0, one launch (start us, length us, event | category | flops | bytes accessed | tf_op | source)
XLA Modules:
  0.0 23.6 jit_solution(6855850867987203379)
XLA Ops:
  0.6 21.0 %fused_block.1 = (bf16[64,2048]{1,0:T(8,128)(2,1)S(1)}, bf16[480,2048]{1,0:T(8,128)(2,1)S(1)}) custom-call(bf16[64,2048]{1,0:T(8,128)(2,1)} %x_ref.1, bf16[2048,2048]{1,0:T(8,128)(2,1)} %wq.1, bf16[2048,2048]{1,0:T(8,128)(2,1)} %wk.1, bf16[2048,2048]{1,0:T(8,128)(2,1)} %wv.1, bf16[2048,2048]{1,0:T(8,128)(2,1)} %wo.1, bf16[2048,2048]{1,0:T(8,128)(2,1)} %wg.1, ...), custom_call_target="tpu_custom_call" | custom-call | flops 6000000000 | bytes 36000000 | tf_op jit(solution)/shard_map/fused_block/pallas_call | solution.py:254
  21.7 0.7 %copy.14 = bf16[64,2048]{1,0:T(8,128)(2,1)} copy(bf16[64,2048]{1,0:T(8,128)(2,1)S(1)} %get-tuple-element.6) | data formatting | bytes 524288
  22.4 1.3 %copy.15 = bf16[15,32,2048]{2,1,0:T(8,128)(2,1)} copy(bf16[15,32,2048]{2,1,0:T(8,128)(2,1)S(1)} %bitcast.3) | data formatting | bytes 3932160
